TPU v7x, 256 devices: a whole 4x4x8 slice. The times are simulated.
256 devices in a mesh: feat: 64 (over y, z, core), samp: 4 (over x).
Axes of the slice: x: 4, y: 4, z: 8, core: 2. Of those that a mesh axis runs over, the one named last changes fastest.
Arguments:
- design: bfloat16 [14336, 65536], P('samp', 'feat'), may hold values from -0.125 to 0.125
- targets: bfloat16 [14336, 128], P('samp'), may hold values from -26 to 26
- warm_start: float32 [65536, 128], P('feat'), may hold values from -0.6 to 0.6
- active_mask: int32 [2, 65536], P(None, 'feat'), may hold values 0 or 1
- penalty_index: int32 [1], replicated, may hold values from 0 to 7
Outputs:
- coefficients: float32 [65536, 128], P('feat')
- correlations: float32 [3, 65536], P(None, 'feat')
- relative_gaps: float32 [3], replicated
- pruned_counts: float32 [2], replicated
All inputs are finite; a program needn't handle non-finite values. No bound on the sum of `active_mask` on one device may be relied on, other than what follows from the above.
Results may differ from a plain program's by a relative error of at most 0.0024.
The roundings to bfloat16 on the way count: a program that leaves them out, or rounds other values in their place, can miss the bound.
Values may be sent and summed in bfloat16 or wider, within the bound.
A program may use at most 64 MiB of HBM per device.

v0:
```python
import jax
import jax.numpy as jnp
from jax import lax
from jax.sharding import Mesh
from jax.sharding import PartitionSpec as P

ITERS = 2
FEAT = ("feat_0", "feat_1", "feat_2")
FEAT_SAMP = ("feat_0", "feat_1", "feat_2", "samp")


def copy_for_each(value, axis):
    copies = jnp.broadcast_to(value, (lax.axis_size(axis), *value.shape))
    return lax.all_to_all(copies, axis, split_axis=0, concat_axis=0, tiled=True)


def of_everyone(value, axis):
    return copy_for_each(value, axis).sum(axis=0)


def packed_total(arrays, axis):
    ends = [0]
    for a in arrays:
        ends.append(ends[-1] + a.size)
    running = of_everyone(jnp.concatenate([a.ravel() for a in arrays]), axis)
    return tuple((running[b:e].reshape(a.shape) for a, b, e in zip(arrays, ends, ends[1:])))


def of_everyone_2(value, axis):
    return copy_for_each(value, axis).max(axis=0)


def in_blocks(value, dim, size):
    before, after = (value.shape[:dim], value.shape[dim + 1 :])
    return jnp.moveaxis(value.reshape(*before, size, -1, *after), dim, 0)


def sent_and_summed(value, axis, dim):
    parts = in_blocks(value, dim, lax.axis_size(axis))
    arrived = lax.all_to_all(parts, axis, split_axis=0, concat_axis=0, tiled=True)
    return arrived.sum(axis=0)


def joined_along(parts, dim):
    lengths = list(parts.shape[1:])
    lengths[dim] *= parts.shape[0]
    return jnp.moveaxis(parts, 0, dim).reshape(lengths)


def collect(value, axis, dim):
    return joined_along(copy_for_each(value, axis), dim)


def by_axis(value, axes):
    for axis in axes:
        value = lax.psum(value, axis)
    return value


def group_norms(matrix):
    return jnp.sqrt(jnp.sum(matrix * matrix, axis=1))


def transpose_product(design, right_side):
    return lax.dot_general(
        design, right_side, (((0,), (0,)), ((), ())), preferred_element_type=jnp.float32
    )


def local(design, targets, warm_start, active_mask, penalty_index):
    row_count, col_count = design.shape
    feat_size = lax.axis_size(FEAT)
    feat_slot = lax.axis_index(FEAT)
    block_rows = row_count // feat_size
    samp_first = (lax.axis_index("samp") == 0).astype(jnp.float32)
    corr_local = transpose_product(design, targets)
    squares_local = jnp.sum(jnp.square(design.astype(jnp.float32)), axis=0)
    corr_y, column_squares = packed_total((corr_local, squares_local), "samp")
    penalty_max = of_everyone_2(jnp.max(group_norms(corr_y)), FEAT)
    penalty = penalty_max / (8.0 + 4.0 * penalty_index[0].astype(jnp.float32))
    step_sizes = 0.5 / (1.0 + column_squares)
    current = warm_start
    correlations = []
    relative_gaps = []
    pruned_counts = []
    own_targets = lax.dynamic_slice_in_dim(targets, feat_slot * block_rows, block_rows, 0)
    for iteration in range(ITERS + 1):
        current_half = current.astype(jnp.bfloat16)
        fitted = sent_and_summed(
            jnp.dot(design, current_half, preferred_element_type=jnp.float32), FEAT, 0
        )
        residual = (own_targets.astype(jnp.float32) - fitted).astype(jnp.bfloat16)
        grad_local = transpose_product(design, collect(residual, FEAT, 0))
        resid_float = residual.astype(jnp.float32)
        rr_local = jnp.sum(resid_float * resid_float)
        ry_local = jnp.sum(resid_float * own_targets.astype(jnp.float32))
        bn_local = samp_first * jnp.sum(group_norms(current))
        if iteration < ITERS:
            keep = active_mask[iteration].astype(jnp.float32)
            pruned_local = samp_first * jnp.sum(1.0 - keep)
        else:
            pruned_local = jnp.zeros((), jnp.float32)
        gradient = of_everyone(grad_local, "samp")
        grad_norms = group_norms(gradient)
        local_max = jnp.max(grad_norms)
        grad_top = of_everyone_2(local_max, FEAT)
        rr_sum, ry_sum, bn_sum, pruned_sum = (
            by_axis(rr_local, FEAT_SAMP),
            by_axis(ry_local, FEAT_SAMP),
            by_axis(bn_local, FEAT_SAMP),
            by_axis(pruned_local, FEAT_SAMP),
        )
        scale = jnp.maximum(penalty, grad_top)
        correlations.append(grad_norms / scale)
        primal = 0.5 * rr_sum + penalty * bn_sum
        ratio = penalty / scale
        dual = ratio * ry_sum - 0.5 * ratio * ratio * rr_sum
        relative_gaps.append((primal - dual) / (primal + 1.0))
        if iteration < ITERS:
            pruned_counts.append(pruned_sum)
            moved = current + step_sizes[:, None] * gradient
            moved_norms = group_norms(moved)
            cutoff = step_sizes * penalty
            factor = jnp.maximum(moved_norms - cutoff, 0.0) / jnp.maximum(moved_norms, cutoff)
            current = (keep * factor)[:, None] * moved
    return (current, jnp.stack(correlations), jnp.stack(relative_gaps), jnp.stack(pruned_counts))


def solution(mesh):
    torus = Mesh(
        mesh.devices.reshape(4, 8, 2, mesh.shape["samp"]), ("feat_0", "feat_1", "feat_2", "samp")
    )
    in_specs = (P("samp", FEAT), P("samp", None), P(FEAT, None), P(None, FEAT), P())
    out_specs = (P(FEAT, None), P(None, FEAT), P(), P())
    return jax.shard_map(local, mesh=torus, in_specs=in_specs, out_specs=out_specs, check_vma=False)
```

profile of v0, /device:TPU:1, one launch (start us, length us, event | category | flops | bytes accessed | tf_op | source)
XLA Modules:
  0.0 521.2 jit_solution(8064084640023801377)
XLA Ops:
  0.6 6.5 %fusion.4 = f32[3584,128]{1,0:T(8,128)} fusion(bf16[3584,1024]{1,0:T(8,128)(2,1)} %param.5, f32[1024,128]{1,0:T(8,128)} %param.7), kind=kOutput, calls=%fused_computation.25 | convolution fusion | flops 939655168 | bytes 9699328 | tf_op jit(solution)/shard_map/dot_general | solution.py:90
  7.2 13.1 %all-to-all-start.1 = ((f32[64,56,128]{2,1,0:T(8,128)}), f32[64,56,128]{2,1,0:T(8,128)S(1)}, u32[]{:S(2)}, u32[]{:S(2)}) async-start(f32[64,56,128]{2,1,0:T(8,128)} %bitcast.3), calls=%async_computation.1 | async-start | bytes 3670016 | tf_op jit(solution)/shard_map/all_to_all | solution.py:40
  30.1 35.6 %all-to-all-done.1 = f32[64,56,128]{2,1,0:T(8,128)S(1)} async-done(((f32[64,56,128]{2,1,0:T(8,128)}), f32[64,56,128]{2,1,0:T(8,128)S(1)}, u32[]{:S(2)}, u32[]{:S(2)}) %all-to-all-start.1) | async-done | bytes 1835040 | tf_op jit(solution)/shard_map/all_to_all | solution.py:40
  75.5 23.6 %all-to-all-done = f32[4,1,132096]{2,1,0:T(1,128)S(1)} async-done(((f32[4,1,132096]{2,1,0:T(1,128)}), f32[4,1,132096]{2,1,0:T(1,128)S(1)}, u32[]{:S(2)}, u32[]{:S(2)}) %all-to-all-start) | async-done | bytes 2113568 | tf_op jit(solution)/shard_map/all_to_all | solution.py:14
  100.2 7.1 %all-to-all-start.2 = ((bf16[64,56,128]{2,1,0:T(8,128)(2,1)}), bf16[64,56,128]{2,1,0:T(8,128)(2,1)S(1)}, u32[]{:S(2)}, u32[]{:S(2)}) async-start(bf16[64,56,128]{2,1,0:T(8,128)(2,1)} %broadcast_in_dim.38), calls=%async_computation.2 | async-start | bytes 1835008 | tf_op jit(solution)/shard_map/all_to_all | solution.py:14
  114.3 18.6 %all-to-all-done.2 = bf16[64,56,128]{2,1,0:T(8,128)(2,1)S(1)} async-done(((bf16[64,56,128]{2,1,0:T(8,128)(2,1)}), bf16[64,56,128]{2,1,0:T(8,128)(2,1)S(1)}, u32[]{:S(2)}, u32[]{:S(2)}) %all-to-all-start.2) | async-done | bytes 917536 | tf_op jit(solution)/shard_map/all_to_all | solution.py:14
  134.2 6.2 %all-to-all-start.4 = ((f32[64,1,1]{2,1,0:T(1,128)}), f32[64,1,1]{2,1,0:T(1,128)S(1)}, u32[]{:S(2)}, u32[]{:S(2)}) async-start(f32[64,1,1]{2,1,0:T(1,128)} %broadcast_in_dim.40), calls=%async_computation.4 | async-start | bytes 65536 | tf_op jit(solution)/shard_map/all_to_all | solution.py:14
  157.5 23.0 %all-to-all-done.3 = f32[4,1024,128]{2,1,0:T(8,128)S(1)} async-done(((f32[4,1024,128]{2,1,0:T(8,128)}), f32[4,1024,128]{2,1,0:T(8,128)S(1)}, u32[]{:S(2)}, u32[]{:S(2)}) %all-to-all-start.3) | async-done | bytes 2097184 | tf_op jit(solution)/shard_map/all_to_all | solution.py:14
  182.6 7.1 %convolution_bitcast_fusion.2 = f32[3584,128]{0,1:T(8,128)} fusion(bf16[3584,1024]{1,0:T(8,128)(2,1)} %param.5, f32[1024,128]{1,0:T(8,128)S(1)} %get-tuple-element.61, f32[1024]{0:T(1024)S(1)} %get-tuple-element.67), kind=kOutput, calls=%fused_computation.3 | convolution fusion | flops 939786240 | bytes 9703424 | tf_op jit(solution)/shard_map/dot_general | solution.py:90
  191.6 52.0 %all_to_all.75 = f32[64,56,128]{2,1,0:T(8,128)} all-to-all(f32[64,56,128]{2,1,0:T(8,128)S(1)} %bitcast.48), channel_id=1, replica_groups=mesh['feat_0'=4,'feat_1'=8,'feat_2'=2,'samp'=4] {'feat_0','feat_1','feat..., dimensions={0} | all-to-all | bytes 3670016 | tf_op jit(solution)/shard_map/all_to_all | solution.py:40
  246.0 31.5 %all_to_all.76 = bf16[64,56,128]{2,1,0:T(8,128)(2,1)S(1)} all-to-all(bf16[64,56,128]{2,1,0:T(8,128)(2,1)S(1)} %broadcast_in_dim.41), channel_id=1, replica_groups=mesh['feat_0'=4,'feat_1'=8,'feat_2'=2,'samp'=4] {'feat_0','feat_1','feat..., dimensions={0} | all-to-all | bytes 1835008 | tf_op jit(solution)/shard_map/all_to_all | solution.py:14
  282.2 28.6 %all_to_all.77 = f32[4,1024,128]{2,1,0:T(8,128)S(1)} all-to-all(f32[4,1024,128]{2,1,0:T(8,128)S(1)} %broadcast_in_dim.42), channel_id=1, replica_groups=mesh['feat_0'=4,'feat_1'=8,'feat_2'=2,'samp'=4] {'samp'}, dimensions={0} | all-to-all | bytes 4194304 | tf_op jit(solution)/shard_map/all_to_all | solution.py:14
  321.3 6.8 %all-to-all-start.10 = ((f32[64,56,128]{2,1,0:T(8,128)}), f32[64,56,128]{2,1,0:T(8,128)S(1)}, u32[]{:S(2)}, u32[]{:S(2)}) async-start(f32[64,56,128]{2,1,0:T(8,128)} %bitcast.47), calls=%async_computation.10 | async-start | bytes 3670016 | tf_op jit(solution)/shard_map/all_to_all | solution.py:40
  328.7 44.8 %all-to-all-done.10 = f32[64,56,128]{2,1,0:T(8,128)S(1)} async-done(((f32[64,56,128]{2,1,0:T(8,128)}), f32[64,56,128]{2,1,0:T(8,128)S(1)}, u32[]{:S(2)}, u32[]{:S(2)}) %all-to-all-start.10) | async-done | bytes 1835040 | tf_op jit(solution)/shard_map/all_to_all | solution.py:40
  374.7 6.0 %all-to-all-start.8 = ((f32[64,1,1]{2,1,0:T(1,128)}), f32[64,1,1]{2,1,0:T(1,128)S(1)}, u32[]{:S(2)}, u32[]{:S(2)}) async-start(f32[64,1,1]{2,1,0:T(1,128)} %broadcast_in_dim.43), calls=%async_computation.8 | async-start | bytes 65536 | tf_op jit(solution)/shard_map/all_to_all | solution.py:14
  382.2 7.8 %all-to-all-done.8 = f32[64,1,1]{2,1,0:T(1,128)S(1)} async-done(((f32[64,1,1]{2,1,0:T(1,128)}), f32[64,1,1]{2,1,0:T(1,128)S(1)}, u32[]{:S(2)}, u32[]{:S(2)}) %all-to-all-start.8) | async-done | bytes 288 | tf_op jit(solution)/shard_map/all_to_all | solution.py:14
  396.4 25.1 %all-to-all-done.11 = bf16[64,56,128]{2,1,0:T(8,128)(2,1)S(1)} async-done(((bf16[64,56,128]{2,1,0:T(8,128)(2,1)}), bf16[64,56,128]{2,1,0:T(8,128)(2,1)S(1)}, u32[]{:S(2)}, u32[]{:S(2)}) %all-to-all-start.11) | async-done | bytes 917536 | tf_op jit(solution)/shard_map/all_to_all | solution.py:14
  422.7 6.3 %all-to-all-start.9 = ((f32[64,1,1]{2,1,0:T(1,128)}), f32[64,1,1]{2,1,0:T(1,128)S(1)}, u32[]{:S(2)}, u32[]{:S(2)}) async-start(f32[64,1,1]{2,1,0:T(1,128)} %broadcast_in_dim.44), calls=%async_computation.9 | async-start | bytes 65536 | tf_op jit(solution)/shard_map/all_to_all | solution.py:14
  452.4 7.9 %all-reduce.2 = (f32[]{:T(128)}, f32[]{:T(128)}, f32[]{:T(128)}, f32[]{:T(128)}, f32[]{:T(128)}, /*index=5*/f32[]{:T(128)}, f32[]{:T(128)}, f32[]{:T(128)}, f32[]{:T(128)}, f32[]{:T(128)}, /*index=10*/f32[]{:T(128)}) all-reduce(f32[]{:T(128)} %get-tuple-element.11, ...), channel_id=1, replica_groups=mesh['feat_0'=4,'feat_1'=8,'feat_2'=2,'samp'=4] {'feat_0'}, use_global_device_ids=true, to_apply=%region_55.0 | all-reduce | flops 11 | bytes 88 | tf_op jit(solution)/shard_map/psum | solution.py:56
  460.3 12.6 %all-reduce = (f32[]{:T(128)}, f32[]{:T(128)}, f32[]{:T(128)}, f32[]{:T(128)}, f32[]{:T(128)}, /*index=5*/f32[]{:T(128)}, f32[]{:T(128)}, f32[]{:T(128)}, f32[]{:T(128)}, f32[]{:T(128)}, /*index=10*/f32[]{:T(128)}) all-reduce(f32[]{:T(128)} %get-tuple-element.35, ...), channel_id=1, replica_groups=mesh['feat_0'=4,'feat_1'=8,'feat_2'=2,'samp'=4] {'feat_1'}, use_global_device_ids=true, to_apply=%region_56.0 | all-reduce | flops 11 | bytes 88 | tf_op jit(solution)/shard_map/psum | solution.py:56
  472.9 8.4 %all-reduce.3 = (f32[]{:T(128)}, f32[]{:T(128)}, f32[]{:T(128)}, f32[]{:T(128)}, f32[]{:T(128)}, /*index=5*/f32[]{:T(128)}, f32[]{:T(128)}, f32[]{:T(128)}, f32[]{:T(128)}, f32[]{:T(128)}, /*index=10*/f32[]{:T(128)}) all-reduce(f32[]{:T(128)} %get-tuple-element.13, ...), channel_id=1, replica_groups=mesh['feat_0'=4,'feat_1'=8,'feat_2'=2,'samp'=4] {'feat_2'}, use_global_device_ids=true, to_apply=%region_57.0 | all-reduce | flops 11 | bytes 88 | tf_op jit(solution)/shard_map/psum | solution.py:56
  481.3 9.7 %all-reduce.1 = (f32[]{:T(128)}, f32[]{:T(128)}, f32[]{:T(128)}, f32[]{:T(128)}, f32[]{:T(128)}, /*index=5*/f32[]{:T(128)}, f32[]{:T(128)}, f32[]{:T(128)}, f32[]{:T(128)}, f32[1]{0:T(128)}, /*index=10*/f32[1]{0:T(128)}) all-reduce(f32[]{:T(128)} %get-tuple-element.46, ...), channel_id=1, replica_groups=mesh['feat_0'=4,'feat_1'=8,'feat_2'=2,'samp'=4] {'samp'}, use_global_device_ids=true, to_apply=%region_58.0 | all-reduce | flops 11 | bytes 88 | tf_op jit(solution)/shard_map/psum | solution.py:56
  499.9 7.4 %all-to-all-start.13 = ((f32[64,1,1]{2,1,0:T(1,128)}), f32[64,1,1]{2,1,0:T(1,128)S(1)}, u32[]{:S(2)}, u32[]{:S(2)}) async-start(f32[64,1,1]{2,1,0:T(1,128)} %broadcast_in_dim.47), calls=%async_computation.13 | async-start | bytes 65536 | tf_op jit(solution)/shard_map/all_to_all | solution.py:14
  508.6 7.9 %all-to-all-done.13 = f32[64,1,1]{2,1,0:T(1,128)S(1)} async-done(((f32[64,1,1]{2,1,0:T(1,128)}), f32[64,1,1]{2,1,0:T(1,128)S(1)}, u32[]{:S(2)}, u32[]{:S(2)}) %all-to-all-start.13) | async-done | bytes 288 | tf_op jit(solution)/shard_map/all_to_all | solution.py:14
  (76 shorter events, 100.6 us)
Async XLA Ops:
  0.6 19.7 %copy-start.4 = (bf16[3584,128]{1,0:T(8,128)(2,1)S(1)}, bf16[3584,128]{1,0:T(8,128)(2,1)}, u32[]{:S(2)}) copy-start(bf16[3584,128]{1,0:T(8,128)(2,1)} %param.6) | copy-start | bytes 2752516
  7.2 58.5 %all-to-all-start.1 = ((f32[64,56,128]{2,1,0:T(8,128)}), f32[64,56,128]{2,1,0:T(8,128)S(1)}, u32[]{:S(2)}, u32[]{:S(2)}) async-start(f32[64,56,128]{2,1,0:T(8,128)} %bitcast.3), calls=%async_computation.1 | async-start | bytes 3670016 | tf_op jit(solution)/shard_map/all_to_all | solution.py:40
  65.7 3.5 copy-start
  69.2 30.0 %all-to-all-start = ((f32[4,1,132096]{2,1,0:T(1,128)}), f32[4,1,132096]{2,1,0:T(1,128)S(1)}, u32[]{:S(2)}, u32[]{:S(2)}) async-start(f32[4,1,132096]{2,1,0:T(1,128)} %broadcast_in_dim.37), calls=%async_computation | async-start | bytes 4227072 | tf_op jit(solution)/shard_map/all_to_all | solution.py:14
  100.2 32.8 %all-to-all-start.2 = ((bf16[64,56,128]{2,1,0:T(8,128)(2,1)}), bf16[64,56,128]{2,1,0:T(8,128)(2,1)S(1)}, u32[]{:S(2)}, u32[]{:S(2)}) async-start(bf16[64,56,128]{2,1,0:T(8,128)(2,1)} %broadcast_in_dim.38), calls=%async_computation.2 | async-start | bytes 1835008 | tf_op jit(solution)/shard_map/all_to_all | solution.py:14
  134.2 15.5 %all-to-all-start.4 = ((f32[64,1,1]{2,1,0:T(1,128)}), f32[64,1,1]{2,1,0:T(1,128)S(1)}, u32[]{:S(2)}, u32[]{:S(2)}) async-start(f32[64,1,1]{2,1,0:T(1,128)} %broadcast_in_dim.40), calls=%async_computation.4 | async-start | bytes 65536 | tf_op jit(solution)/shard_map/all_to_all | solution.py:14
  144.7 10.8 %copy-start.3 = (s32[2,1024]{1,0:T(2,128)S(1)}, s32[2,1024]{1,0:T(2,128)}, u32[]{:S(2)}) copy-start(s32[2,1024]{1,0:T(2,128)} %param.8) | copy-start | bytes 24580
  144.7 36.0 %copy-start.1 = (f32[1024,128]{1,0:T(8,128)S(1)}, f32[1024,128]{1,0:T(8,128)}, u32[]{:S(2)}) copy-start(f32[1024,128]{1,0:T(8,128)} %param.7) | copy-start | bytes 1572868
  151.2 29.3 %all-to-all-start.3 = ((f32[4,1024,128]{2,1,0:T(8,128)}), f32[4,1024,128]{2,1,0:T(8,128)S(1)}, u32[]{:S(2)}, u32[]{:S(2)}) async-start(f32[4,1024,128]{2,1,0:T(8,128)} %broadcast_in_dim.39), calls=%async_computation.3 | async-start | bytes 4194304 | tf_op jit(solution)/shard_map/all_to_all | solution.py:14
  313.7 7.6 %copy-start.2 = (f32[1024,128]{1,0:T(8,128)}, f32[1024,128]{1,0:T(8,128)S(1)}, u32[]{:S(2)}) copy-start(f32[1024,128]{1,0:T(8,128)S(1)} %get-tuple-element.58) | copy-start | bytes 1572868
  321.3 52.2 %all-to-all-start.10 = ((f32[64,56,128]{2,1,0:T(8,128)}), f32[64,56,128]{2,1,0:T(8,128)S(1)}, u32[]{:S(2)}, u32[]{:S(2)}) async-start(f32[64,56,128]{2,1,0:T(8,128)} %bitcast.47), calls=%async_computation.10 | async-start | bytes 3670016 | tf_op jit(solution)/shard_map/all_to_all | solution.py:40
  374.7 15.3 %all-to-all-start.8 = ((f32[64,1,1]{2,1,0:T(1,128)}), f32[64,1,1]{2,1,0:T(1,128)S(1)}, u32[]{:S(2)}, u32[]{:S(2)}) async-start(f32[64,1,1]{2,1,0:T(1,128)} %broadcast_in_dim.43), calls=%async_computation.8 | async-start | bytes 65536 | tf_op jit(solution)/shard_map/all_to_all | solution.py:14
  391.0 30.5 %all-to-all-start.11 = ((bf16[64,56,128]{2,1,0:T(8,128)(2,1)}), bf16[64,56,128]{2,1,0:T(8,128)(2,1)S(1)}, u32[]{:S(2)}, u32[]{:S(2)}) async-start(bf16[64,56,128]{2,1,0:T(8,128)(2,1)} %broadcast_in_dim.45), calls=%async_computation.11 | async-start | bytes 1835008 | tf_op jit(solution)/shard_map/all_to_all | solution.py:14
  422.7 15.6 %all-to-all-start.9 = ((f32[64,1,1]{2,1,0:T(1,128)}), f32[64,1,1]{2,1,0:T(1,128)S(1)}, u32[]{:S(2)}, u32[]{:S(2)}) async-start(f32[64,1,1]{2,1,0:T(1,128)} %broadcast_in_dim.44), calls=%async_computation.9 | async-start | bytes 65536 | tf_op jit(solution)/shard_map/all_to_all | solution.py:14
  439.8 57.8 %all-to-all-start.12 = ((f32[4,1024,128]{2,1,0:T(8,128)}), f32[4,1024,128]{2,1,0:T(8,128)S(1)}, u32[]{:S(2)}, u32[]{:S(2)}) async-start(f32[4,1024,128]{2,1,0:T(8,128)} %broadcast_in_dim.46), calls=%async_computation.12 | async-start | bytes 4194304 | tf_op jit(solution)/shard_map/all_to_all | solution.py:14
  499.9 16.7 %all-to-all-start.13 = ((f32[64,1,1]{2,1,0:T(1,128)}), f32[64,1,1]{2,1,0:T(1,128)S(1)}, u32[]{:S(2)}, u32[]{:S(2)}) async-start(f32[64,1,1]{2,1,0:T(1,128)} %broadcast_in_dim.47), calls=%async_computation.13 | async-start | bytes 65536 | tf_op jit(solution)/shard_map/all_to_all | solution.py:14
where the time goes:
time: 523 us; the launch traced here: 521 us
  waiting for transfers between devices  196 us (37%)
  blocking collectives  151 us (29%)
  starting transfers between devices  68.8 us (13%)
  matrix products  37.4 us (7%)
  other arithmetic  33.5 us (6%)
  local copies, waits for them, and re-layouts  17.8 us (3%)
  between operations  16.9 us (3%)
    all_to_all x9, waiting for transfers between devices, copy_for_each(): return lax.all_to_all(copies, axis, split_axis=0, concat_axis=0, tiled=True)  116 us
    all_to_all x2, waiting for transfers between devices, sent_and_summed(): lax.all_to_all(parts, axis, split_axis=0, concat_axis=0, tiled=True)  80.3 us
    all_to_all x2, blocking collectives, copy_for_each(): return lax.all_to_all(copies, axis, split_axis=0, concat_axis=0, tiled=True)  60.1 us
    all_to_all x1, blocking collectives, sent_and_summed(): lax.all_to_all(parts, axis, split_axis=0, concat_axis=0, tiled=True)  52 us
    all_to_all x9, starting transfers between devices, copy_for_each(): return lax.all_to_all(copies, axis, split_axis=0, concat_axis=0, tiled=True)  48.9 us
    psum x4, blocking collectives, by_axis(): value = lax.psum(value, axis)  38.6 us
    all_to_all x2, starting transfers between devices, sent_and_summed(): lax.all_to_all(parts, axis, split_axis=0, concat_axis=0, tiled=True)  19.9 us
    dot_general x3, matrix products, local(): jnp.dot(design, current_half, preferred_element_type=jnp.float32)  19.5 us
  transfers between devices with their start and end apart: 11, of which 10 were waited for; matrix products, arithmetic and copies ran while one was open for 7% of the time, Pallas kernels for 0%

commit v1 on v0

v1 whole, which is shorter than its diff:
```python
import jax
import jax.numpy as jnp
from jax import lax
from jax.experimental import pallas as pl
from jax.experimental.pallas import tpu as pltpu
from jax.sharding import Mesh
from jax.sharding import PartitionSpec as P

ITERS = 2
NY, NZ, NX = 4, 8, 4
MESH = pl.DeviceIdType.MESH
F32 = jnp.float32
BF16 = jnp.bfloat16
Y_TYPES = (BF16, F32, BF16)
Z_TYPES = (BF16, F32, BF16)
X_TYPES = (F32, F32, BF16, BF16)


def lanes_folded(row, op):
    return op(row[:, :128], row[:, 128:])


def column_norms(matrix):
    return jnp.sqrt(jnp.sum(matrix * matrix, axis=0, keepdims=True))


def kernel(
    design, targets, target_blocks, warm, mask, penalty_index,
    coef, corr, gaps, counts,
    D, T, own_targets, half, cs, cr, ys, yr, keep, zt, zs, zr, R, G, gs, gr,
    current, coef_parts, cqs, cqr, pen_src, pen_z, pen_y, pen_c, pen_x,
    norms, fin_src, fin_x, fin_c, fin_y, fin_z, stats, load_sem, send_sem, recv_sem,
):
    y, z, c, x = (lax.axis_index(a) for a in ("y", "z", "c", "x"))
    oc = 1 - c
    step = 1 - 2 * c
    yf, yb, y2 = lax.rem(y + step + NY, NY), lax.rem(y - step + NY, NY), lax.rem(y + 2, NY)
    xf, xb, x2 = lax.rem(x + step + NX, NX), lax.rem(x - step + NX, NX), lax.rem(x + 2, NX)
    block = D.shape[0] // (2 * NY)
    quarter = D.shape[1] // NX
    sub = block // NZ
    task_count = warm.shape[1]

    def rows(cc, yy):
        return pl.ds(pl.multiple_of((cc * NY + yy) * block, block), block)

    def cols(xx):
        return pl.ds(pl.multiple_of(xx * quarter, quarter), quarter)

    used = [0]
    pending = []

    def send(src, dst, device):
        i = used[0]
        used[0] += 1
        copy = pltpu.make_async_remote_copy(
            src_ref=src, dst_ref=dst, send_sem=send_sem.at[i], recv_sem=recv_sem.at[i],
            device_id=device, device_id_type=MESH,
        )
        copy.start()
        pending.append(copy)
        return copy

    def drain():
        for copy in pending:
            copy.wait_send()
        pending.clear()

    def to_all(src, dst, axis, me, n):
        return [
            send(src, dst.at[d - 1], {axis: lax.rem(me + d, n)}) for d in range(1, n)
        ]

    def waited(copies):
        for copy in copies:
            copy.wait_recv()

    others, mine = (y2, yf, yb, y), (y2, yb, yf, y)
    steps = (("o", 0), ("o", 1), ("m", 0), ("o", 2), ("m", 1), ("o", 3), ("m", 2), ("m", 3))
    loads = {}
    for i, (kind, j) in enumerate(steps):
        cc, yy = (oc, others[j]) if kind == "o" else (c, mine[j])
        load = pltpu.make_async_copy(design.at[rows(cc, yy), :], D.at[rows(cc, yy), :], load_sem.at[i])
        load.start()
        loads[kind, j] = load
    own_load = pltpu.make_async_copy(
        target_blocks.at[(c * NY + y) * NZ + z], own_targets, load_sem.at[8]
    )
    own_load.start()
    target_load = pltpu.make_async_copy(targets, T, load_sem.at[9])
    target_load.start()

    barrier = pltpu.get_barrier_semaphore()
    peers = (
        [{"c": oc}]
        + [{"y": lax.rem(y + d, NY)} for d in range(1, NY)]
        + [{"z": lax.rem(z + d, NZ)} for d in range(1, NZ)]
        + [{"x": lax.rem(x + d, NX)} for d in range(1, NX)]
    )
    for peer in peers:
        pl.semaphore_signal(barrier, inc=1, device_id=peer, device_id_type=MESH)

    half[0] = warm[...].astype(BF16).reshape(half.shape[1:])
    current[...] = warm[cols(x), :].T
    bn = [column_norms(current[...])]
    pl.semaphore_wait(barrier, len(peers))

    def grad_block(R_t, cc, yy, first):
        part = R_t[cc, yy].astype(F32).reshape(block, task_count).astype(BF16)
        product = lax.dot_general(
            part, D[rows(cc, yy), :], (((0,), (0,)), ((), ())), preferred_element_type=F32
        )
        if first:
            G[...] = product
        else:
            G[...] += product

    def ring_start(k):
        gs[k][0] = G[:, cols(x2)].astype(X_TYPES[k])
        a = send(gs[k].at[0], gr[k].at[0], {"x": xf})
        gs[k][1] = G[:, cols(xb)].astype(X_TYPES[k])
        b = send(gs[k].at[1], gr[k].at[1], {"x": xb})
        return a, b

    def ring_middle(k, a):
        a.wait_recv()
        gs[k][2] = (G[:, cols(xf)] + gr[k][0].astype(F32)).astype(X_TYPES[k])
        return send(gs[k].at[2], gr[k].at[2], {"x": xf})

    def ring_end(k, b, last):
        b.wait_recv()
        last.wait_recv()
        return G[:, cols(x)] + gr[k][1].astype(F32) + gr[k][2].astype(F32)

    def maximum_of(src, arrived):
        value = src
        for d in range(arrived.shape[0]):
            value = jnp.maximum(value, arrived[d])
        return value

    penalty = step_sizes = None
    coef_copies = []
    rr, ry, pruned = [], [], []
    for t in range(ITERS + 1):
        weights = half[t].reshape(D.shape[1], task_count)

        def product(cc, yy):
            return jnp.dot(D[rows(cc, yy), :], weights, preferred_element_type=F32)

        core_copies = []

        def other(j):
            if t == 0:
                loads["o", j].wait()
            cs[j] = product(oc, others[j])
            core_copies.append(send(cs.at[j], cr.at[t, j], {"c": oc}))

        def summed(j):
            if t == 0:
                loads["m", j].wait()
            own = product(c, mine[j])
            core_copies[j].wait_recv()
            return own + cr[t, j]

        other(0)
        other(1)
        ys[t][0] = summed(0).astype(Y_TYPES[t])
        ya = send(ys[t].at[0], yr[t].at[0], {"y": yf})
        other(2)
        ys[t][1] = summed(1).astype(Y_TYPES[t])
        yb_copy = send(ys[t].at[1], yr[t].at[1], {"y": yb})
        other(3)
        keep[0] = summed(2)
        keep[1] = summed(3)
        if t == 0:
            target_load.wait()
            for b in range(2 * NY):
                part = T[b * block : (b + 1) * block, :]
                corr_product = lax.dot_general(
                    part, D[b * block : (b + 1) * block, :], (((0,), (0,)), ((), ())),
                    preferred_element_type=F32,
                )
                if b == 0:
                    G[...] = corr_product
                else:
                    G[...] += corr_product
            ca, cb = ring_start(ITERS + 1)
        ya.wait_recv()
        ys[t][2] = (keep[0] + yr[t][0].astype(F32)).astype(Y_TYPES[t])
        yc = send(ys[t].at[2], yr[t].at[2], {"y": yf})
        if t == 0:
            def square_step(i, total):
                v = D[pl.ds(pl.multiple_of(i * 64, 64), 64), :].astype(F32)
                return total + jnp.sum((v * v).reshape(8, 8, v.shape[1]), axis=0)

            squares = lax.fori_loop(
                0, D.shape[0] // 64, square_step, jnp.zeros((8, D.shape[1]), F32)
            )
            squares = jnp.sum(squares, axis=0, keepdims=True)
            for q in range(NX):
                cqs[q] = jnp.broadcast_to(squares[:, q * quarter : (q + 1) * quarter], (8, quarter))
            square_copies = [
                send(cqs.at[lax.rem(x + d, NX)], cqr.at[d - 1], {"x": lax.rem(x + d, NX)})
                for d in range(1, NX)
            ]
            cc_copy = ring_middle(ITERS + 1, ca)
        yb_copy.wait_recv()
        yc.wait_recv()
        total = (keep[1] + yr[t][1].astype(F32) + yr[t][2].astype(F32)).reshape(NZ, sub, task_count)
        zt[...] = total
        zs[t][...] = total.astype(Z_TYPES[t])
        z_copies = []
        for d in range(1, NZ):
            zz = lax.rem(z + d, NZ)
            z_copies.append(send(zs[t].at[zz], zr[t].at[d - 1], {"z": zz}))
        if t == 0:
            corr_y = ring_end(ITERS + 1, cb, cc_copy)
            top = lanes_folded(column_norms(corr_y), jnp.maximum)
            pen_src[0] = jnp.broadcast_to(top, (8, 128))
            pen_copies = to_all(pen_src.at[0], pen_z, "z", z, NZ)
            own_load.wait()
        waited(z_copies)
        fitted = zt[z]
        for d in range(NZ - 1):
            fitted = fitted + zr[t][d].astype(F32)
        target_float = own_targets[...].astype(F32)
        residual = (target_float - fitted).astype(BF16)
        R[t, c, y, z] = residual
        own_rows = R.at[t, c, y, z]
        r_copies = [send(own_rows, own_rows, {"z": lax.rem(z + d, NZ)}) for d in range(1, NZ)]
        resid_float = residual.astype(F32)
        rr.append(jnp.sum(resid_float * resid_float, axis=0, keepdims=True))
        ry.append(jnp.sum(resid_float * target_float, axis=0, keepdims=True))
        if t == 0:
            waited(pen_copies)
            pen_src[1] = maximum_of(pen_src[0], pen_z)
            pen_copies = to_all(pen_src.at[1], pen_y, "y", y, NY)
        waited(r_copies)

        def block_to(yy, device):
            return send(R.at[t, c, yy], R.at[t, c, yy], device)

        R_t = R.at[t]
        g1 = block_to(y, {"y": yf})
        g2 = block_to(y, {"y": yb})
        q0 = block_to(y, {"c": oc})
        if t == 0:
            waited(pen_copies)
            pen_src[2] = maximum_of(pen_src[1], pen_y)
            pen_copies = to_all(pen_src.at[2], pen_c, "c", c, 2)
        grad_block(R_t, c, y, True)
        q0.wait_recv()
        grad_block(R_t, oc, y, False)
        g1.wait_recv()
        g3 = block_to(yb, {"y": yf})
        q1 = block_to(yb, {"c": oc})
        g2.wait_recv()
        q2 = block_to(yf, {"c": oc})
        if t == 0:
            waited(pen_copies)
            pen_src[3] = maximum_of(pen_src[2], pen_c)
            pen_copies = to_all(pen_src.at[3], pen_x, "x", x, NX)
        grad_block(R_t, c, yb, False)
        grad_block(R_t, c, yf, False)
        q1.wait_recv()
        grad_block(R_t, oc, yf, False)
        g3.wait_recv()
        q3 = block_to(y2, {"c": oc})
        q2.wait_recv()
        grad_block(R_t, oc, yb, False)
        grad_block(R_t, c, y2, False)
        q3.wait_recv()
        grad_block(R_t, oc, y2, False)
        ga, gb = ring_start(t)
        if t == 0:
            waited(pen_copies)
            pen_max = jnp.max(maximum_of(pen_src[3], pen_x), axis=(0, 1), keepdims=True)
            penalty = pen_max / (8.0 + 4.0 * penalty_index[0].astype(F32))
            waited(square_copies)
            total_squares = (cqs[x] + cqr[0] + cqr[1] + cqr[2])[0:1, :]
            step_sizes = 0.5 / (1.0 + total_squares)
        gc = ring_middle(t, ga)
        gradient = ring_end(t, gb, gc)
        drain()
        grad_norms = column_norms(gradient)
        norms[x, t : t + 1, :] = grad_norms
        stats[16 + t : 17 + t, :] = lanes_folded(grad_norms, jnp.maximum)
        if t < ITERS:
            active = mask[t : t + 1, cols(x)].astype(F32)
            pruned.append(1.0 - active)
            moved = current[...] + step_sizes * gradient
            moved_norms = column_norms(moved)
            cutoff = step_sizes * penalty
            factor = jnp.maximum(moved_norms - cutoff, 0.0) / jnp.maximum(moved_norms, cutoff)
            updated = (active * factor) * moved
            flipped = updated.T
            half[t + 1, x] = flipped.astype(BF16)
            own_half = half.at[t + 1, x]
            h1 = send(own_half, own_half, {"x": xf})
            h2 = send(own_half, own_half, {"x": xb})
            current[...] = updated
            bn.append(column_norms(updated))
            if t == ITERS - 1:
                coef_parts[x] = flipped
            h1.wait_recv()
            h3 = send(half.at[t + 1, xb], half.at[t + 1, xb], {"x": xf})
            h2.wait_recv()
            h3.wait_recv()
            if t == ITERS - 1:
                own_coef = coef_parts.at[x]
                coef_copies = [send(own_coef, own_coef, {"x": xq}) for xq in (xf, xb, x2)]

    for i, value in enumerate(rr + ry):
        stats[i : i + 1, :] = value
    for i, value in enumerate(bn + pruned):
        stats[6 + i : 7 + i, :] = lanes_folded(value, jnp.add)
    stats[11:16, :] = jnp.zeros((5, 128), F32)
    stats[19:24, :] = jnp.zeros((5, 128), F32)
    norms[x, 3:8, :] = jnp.zeros((5, quarter), F32)
    own_norms = norms.at[x]
    norm_copies = [send(own_norms, own_norms, {"x": xq}) for xq in (xf, xb, x2)]
    fin_src[0] = stats[...]
    for k, (arrived, axis, me, n) in enumerate(
        ((fin_x, "x", x, NX), (fin_c, "c", c, 2), (fin_y, "y", y, NY), (fin_z, "z", z, NZ))
    ):
        copies = to_all(fin_src.at[k], arrived, axis, me, n)
        if k == 1:
            waited(coef_copies)
            for q in range(NX):
                coef[q * quarter : (q + 1) * quarter, :] = coef_parts[q]
        waited(copies)
        sums, tops = fin_src[k, 0:16, :], fin_src[k, 16:24, :]
        for d in range(n - 1):
            sums = sums + arrived[d, 0:16, :]
            tops = jnp.maximum(tops, arrived[d, 16:24, :])
        if k < 3:
            fin_src[k + 1, 0:16, :] = sums
            fin_src[k + 1, 16:24, :] = tops
    sums = jnp.sum(sums, axis=1, keepdims=True)
    tops = jnp.max(tops, axis=1, keepdims=True)
    waited(norm_copies)
    for t in range(ITERS + 1):
        scale = jnp.maximum(penalty, tops[t : t + 1, :])
        for q in range(NX):
            corr[t : t + 1, q * quarter : (q + 1) * quarter] = norms[q, t : t + 1, :] / scale
        rr_sum, ry_sum, bn_sum = sums[t : t + 1], sums[3 + t : 4 + t], sums[6 + t : 7 + t]
        primal = 0.5 * rr_sum + penalty * bn_sum
        ratio = penalty / scale
        dual = ratio * ry_sum - 0.5 * ratio * ratio * rr_sum
        gaps[t] = jnp.sum((primal - dual) / (primal + 1.0))
    for t in range(ITERS):
        counts[t] = jnp.sum(sums[9 + t : 10 + t])
    drain()
    assert used[0] == send_sem.shape[0], used[0]


def local(design, targets, warm_start, active_mask, penalty_index):
    samples, features = design.shape
    tasks = targets.shape[1]
    block = samples // (2 * NY)
    sub = block // NZ
    quarter = features // NX
    steps = ITERS + 1
    vmem, smem, hbm = pltpu.VMEM, pltpu.SMEM, pl.ANY
    target_blocks = targets.reshape(2 * NY * NZ, sub, tasks)
    scratch = [
        vmem((samples, features), BF16),
        vmem((samples, tasks), BF16),
        vmem((sub, tasks), BF16),
        vmem((steps, NX, quarter, tasks), BF16),
        vmem((4, block, tasks), F32),
        vmem((steps, 4, block, tasks), F32),
        tuple(vmem((3, block, tasks), v) for v in Y_TYPES),
        tuple(vmem((3, block, tasks), v) for v in Y_TYPES),
        vmem((2, block, tasks), F32),
        vmem((NZ, sub, tasks), F32),
        tuple(vmem((NZ, sub, tasks), v) for v in Z_TYPES),
        tuple(vmem((NZ - 1, sub, tasks), v) for v in Z_TYPES),
        vmem((steps, 2, NY, NZ, sub, tasks), BF16),
        vmem((tasks, features), F32),
        tuple(vmem((3, tasks, quarter), v) for v in X_TYPES),
        tuple(vmem((3, tasks, quarter), v) for v in X_TYPES),
        vmem((tasks, quarter), F32),
        vmem((NX, quarter, tasks), F32),
        vmem((NX, 8, quarter), F32),
        vmem((NX - 1, 8, quarter), F32),
        vmem((4, 8, 128), F32),
        vmem((NZ - 1, 8, 128), F32),
        vmem((NY - 1, 8, 128), F32),
        vmem((1, 8, 128), F32),
        vmem((NX - 1, 8, 128), F32),
        vmem((NX, 8, quarter), F32),
        vmem((4, 24, 128), F32),
        vmem((NX - 1, 24, 128), F32),
        vmem((1, 24, 128), F32),
        vmem((NY - 1, 24, 128), F32),
        vmem((NZ - 1, 24, 128), F32),
        vmem((24, 128), F32),
        pltpu.SemaphoreType.DMA((10,)),
        pltpu.SemaphoreType.DMA((139,)),
        pltpu.SemaphoreType.DMA((139,)),
    ]
    return pl.pallas_call(
        kernel,
        out_shape=(
            jax.ShapeDtypeStruct((features, tasks), F32),
            jax.ShapeDtypeStruct((steps, features), F32),
            jax.ShapeDtypeStruct((steps,), F32),
            jax.ShapeDtypeStruct((ITERS,), F32),
        ),
        in_specs=[
            pl.BlockSpec(memory_space=hbm),
            pl.BlockSpec(memory_space=hbm),
            pl.BlockSpec(memory_space=hbm),
            pl.BlockSpec(memory_space=vmem),
            pl.BlockSpec(memory_space=vmem),
            pl.BlockSpec(memory_space=smem),
        ],
        out_specs=(
            pl.BlockSpec(memory_space=vmem),
            pl.BlockSpec(memory_space=vmem),
            pl.BlockSpec(memory_space=smem),
            pl.BlockSpec(memory_space=smem),
        ),
        scratch_shapes=scratch,
        compiler_params=pltpu.CompilerParams(
            collective_id=0, has_side_effects=True, vmem_limit_bytes=60 * 1024 * 1024
        ),
        name="lasso_steps",
    )(design, targets, target_blocks, warm_start, active_mask, penalty_index)


def solution(mesh):
    torus = Mesh(mesh.devices.reshape(NY, NZ, 2, NX), ("y", "z", "c", "x"))
    feat = ("y", "z", "c")
    in_specs = (P("x", feat), P("x", None), P(feat, None), P(None, feat), P())
    out_specs = (P(feat, None), P(None, feat), P(), P())
    return jax.shard_map(local, mesh=torus, in_specs=in_specs, out_specs=out_specs, check_vma=False)
```

time: 523 us -> 174 us (0.33)
  waiting for transfers between devices: 196 us -> 0 us
  Pallas kernels: 0 us -> 167 us
  blocking collectives: 151 us -> 0 us
  starting transfers between devices: 68.8 us -> 0 us
  matrix products: 37.4 us -> 0 us
  other arithmetic: 33.5 us -> 0 us
  between operations: 16.9 us -> 1.29 us
  local copies, waits for them, and re-layouts: 17.8 us -> 5.52 us
    all_to_all x11 -> x0, waiting for transfers between devices: 196 us -> none  [the longest x9 116 us: copy_for_each(): return lax.all_to_all(copies, axis, split_axis=0, concat_axis=0, tiled=True)]
    pallas_call x0 -> x1, Pallas kernels: none -> 167 us  [local(): pl.pallas_call(kernel, out_shape=(jax.ShapeDtypeStruct((features, tasks),...]
    all_to_all x3 -> x0, blocking collectives: 112 us -> none  [the longest x2 60.1 us: copy_for_each(): return lax.all_to_all(copies, axis, split_axis=0, concat_axis=0, tiled=True)]
    all_to_all x11 -> x0, starting transfers between devices: 68.8 us -> none  [the longest x9 48.9 us: copy_for_each(): return lax.all_to_all(copies, axis, split_axis=0, concat_axis=0, tiled=True)]
    psum x4 -> x0, blocking collectives: 38.6 us -> none  [by_axis(): value = lax.psum(value, axis)]
    dot_general x7 -> x0, matrix products: 37.4 us -> none  [the longest x3 19.5 us: local(): jnp.dot(design, current_half, preferred_element_type=jnp.float32)]
    reduce_sum x19 -> x0, other arithmetic: 23 us -> none  [the longest x4 5.66 us: of_everyone(): return copy_for_each(value, axis).sum(axis=0)]
    broadcast_in_dim x11 -> x0, local copies, waits for them, and re-layouts: 13.7 us -> none  [copy_for_each(): copies = jnp.broadcast_to(value, (lax.axis_size(axis), *value.shape))]
  transfers between devices with their start and end apart: 11 -> 0, of which waited for: 10 -> 0; matrix products, arithmetic and copies ran while one was open for 7% -> 0% of each run, Pallas kernels for 0% -> 0%
where the time goes in v1:
time: 174 us
  Pallas kernels  167 us (96%)
  local copies, waits for them, and re-layouts  5.52 us (3%)
    pallas_call x1, Pallas kernels, local(): pl.pallas_call(kernel, out_shape=(jax.ShapeDtypeStruct((features, tasks),...  167 us
    unnamed x4, local copies, waits for them, and re-layouts  5.52 us

profile of v1, /device:TPU:1, one launch (start us, length us, event | category | flops | bytes accessed | tf_op | source)
XLA Modules:
  0.0 174.2 jit_solution(1954851906142422725)
XLA Ops:
  1.3 167.4 %lasso_steps.1 = (f32[1024,128]{1,0:T(8,128)}, f32[3,1024]{1,0:T(4,128)}, f32[3]{0:T(128)}, f32[2]{0:T(128)}) custom-call(bf16[3584,1024]{1,0:T(8,128)(2,1)} %design.1, bf16[3584,128]{1,0:T(8,128)(2,1)} %targets.1, bf16[64,56,128]{2,1,0:T(8,128)(2,1)} %bitcast.1, f32[1024,128]{1,0:T(8,128)} %warm.1, s32[2,1024]{1,0:T(2,128)} %mask.1, s32[1]{0:T(128)S(6)} %copy.13.penalty_index), custom_call_target="tpu_custom_call" | custom-call | tf_op jit(solution)/shard_map/lasso_steps/pallas_call | solution.py:403
  168.7 1.9 %copy.14 = f32[1024,128]{1,0:T(8,128)} copy(f32[1024,128]{1,0:T(8,128)} %get-tuple-element.8) | data formatting | bytes 1048576
  170.5 1.3 copy.15
  171.9 1.2 copy.16
  173.1 1.1 copy.17

commit v2 on v1

--- a/solution.py
+++ b/solution.py
@@ -9,6 +9,7 @@
 ITERS = 2
 NY, NZ, NX = 4, 8, 4
 MESH = pl.DeviceIdType.MESH
+FAR_FIRST = (4, 3, 5, 2, 6, 1, 7)
 F32 = jnp.float32
 BF16 = jnp.bfloat16
 Y_TYPES = (BF16, F32, BF16)
@@ -29,7 +30,7 @@
     coef, corr, gaps, counts,
     D, T, own_targets, half, cs, cr, ys, yr, keep, zt, zs, zr, R, G, gs, gr,
     current, coef_parts, cqs, cqr, pen_src, pen_z, pen_y, pen_c, pen_x,
-    norms, fin_src, fin_x, fin_c, fin_y, fin_z, stats, load_sem, send_sem, recv_sem,
+    norms, fin_src, fin_plane, fin_column, stats, load_sem, send_sem, recv_sem,
 ):
     y, z, c, x = (lax.axis_index(a) for a in ("y", "z", "c", "x"))
     oc = 1 - c
@@ -97,13 +98,23 @@
         + [{"z": lax.rem(z + d, NZ)} for d in range(1, NZ)]
         + [{"x": lax.rem(x + d, NX)} for d in range(1, NX)]
     )
+    plane = [
+        {"x": lax.rem(x + d, NX), "y": lax.rem(y + e, NY)}
+        for d in range(NX) for e in range(NY) if d or e
+    ]
+    column = [
+        {"z": lax.rem(z + d, NZ), "c": lax.rem(c + e, 2)} for d in range(NZ) for e in range(2) if d or e
+    ]
+    peers += [
+        {"x": lax.rem(x + d, NX), "y": lax.rem(y + e, NY)} for d in range(1, NX) for e in range(1, NY)
+    ]
+    peers += [{"z": lax.rem(z + d, NZ), "c": oc} for d in range(1, NZ)]
     for peer in peers:
         pl.semaphore_signal(barrier, inc=1, device_id=peer, device_id_type=MESH)
 
     half[0] = warm[...].astype(BF16).reshape(half.shape[1:])
     current[...] = warm[cols(x), :].T
     bn = [column_norms(current[...])]
-    pl.semaphore_wait(barrier, len(peers))
 
     def grad_block(R_t, cc, yy, first):
         part = R_t[cc, yy].astype(F32).reshape(block, task_count).astype(BF16)
@@ -115,21 +126,26 @@
         else:
             G[...] += product
 
+    task_halves = [pl.ds(h * task_count // 2, task_count // 2) for h in range(2)]
+
     def ring_start(k):
         gs[k][0] = G[:, cols(x2)].astype(X_TYPES[k])
-        a = send(gs[k].at[0], gr[k].at[0], {"x": xf})
+        a = [send(gs[k].at[0, p], gr[k].at[0, p], {"x": xf}) for p in task_halves]
         gs[k][1] = G[:, cols(xb)].astype(X_TYPES[k])
         b = send(gs[k].at[1], gr[k].at[1], {"x": xb})
         return a, b
 
     def ring_middle(k, a):
-        a.wait_recv()
-        gs[k][2] = (G[:, cols(xf)] + gr[k][0].astype(F32)).astype(X_TYPES[k])
-        return send(gs[k].at[2], gr[k].at[2], {"x": xf})
+        last = []
+        for copy, p in zip(a, task_halves):
+            copy.wait_recv()
+            gs[k][2, p, :] = (G[p, cols(xf)] + gr[k][0, p, :].astype(F32)).astype(X_TYPES[k])
+            last.append(send(gs[k].at[2, p], gr[k].at[2, p], {"x": xf}))
+        return last
 
     def ring_end(k, b, last):
         b.wait_recv()
-        last.wait_recv()
+        waited(last)
         return G[:, cols(x)] + gr[k][1].astype(F32) + gr[k][2].astype(F32)
 
     def maximum_of(src, arrived):
@@ -142,17 +158,26 @@
     coef_copies = []
     rr, ry, pruned = [], [], []
     for t in range(ITERS + 1):
-        weights = half[t].reshape(D.shape[1], task_count)
+        weights = half[t].reshape(D.shape[1], task_count).astype(F32).T.astype(BF16)
 
         def product(cc, yy):
-            return jnp.dot(D[rows(cc, yy), :], weights, preferred_element_type=F32)
+            turned = lax.dot_general(
+                weights, D[rows(cc, yy), :], (((1,), (1,)), ((), ())), preferred_element_type=F32
+            )
+            return turned.T
 
         core_copies = []
+
+        def halved(src, dst, device, length):
+            parts = [pl.ds(h * length // 2, length // 2) for h in range(2)]
+            return [send(src.at[p], dst.at[p], device) for p in parts]
 
         def other(j):
             if t == 0:
                 loads["o", j].wait()
             cs[j] = product(oc, others[j])
+            if t == 0 and j == 0:
+                pl.semaphore_wait(barrier, len(peers))
             core_copies.append(send(cs.at[j], cr.at[t, j], {"c": oc}))
 
         def summed(j):
@@ -165,7 +190,7 @@
         other(0)
         other(1)
         ys[t][0] = summed(0).astype(Y_TYPES[t])
-        ya = send(ys[t].at[0], yr[t].at[0], {"y": yf})
+        ya = halved(ys[t].at[0], yr[t].at[0], {"y": yf}, block)
         other(2)
         ys[t][1] = summed(1).astype(Y_TYPES[t])
         yb_copy = send(ys[t].at[1], yr[t].at[1], {"y": yb})
@@ -185,9 +210,12 @@
                 else:
                     G[...] += corr_product
             ca, cb = ring_start(ITERS + 1)
-        ya.wait_recv()
-        ys[t][2] = (keep[0] + yr[t][0].astype(F32)).astype(Y_TYPES[t])
-        yc = send(ys[t].at[2], yr[t].at[2], {"y": yf})
+        yc = []
+        for h in range(2):
+            ya[h].wait_recv()
+            p = pl.ds(h * block // 2, block // 2)
+            ys[t][2, p, :] = (keep[0, p, :] + yr[t][0, p, :].astype(F32)).astype(Y_TYPES[t])
+            yc.append(send(ys[t].at[2, p], yr[t].at[2, p], {"y": yf}))
         if t == 0:
             def square_step(i, total):
                 v = D[pl.ds(pl.multiple_of(i * 64, 64), 64), :].astype(F32)
@@ -205,12 +233,12 @@
             ]
             cc_copy = ring_middle(ITERS + 1, ca)
         yb_copy.wait_recv()
-        yc.wait_recv()
+        waited(yc)
         total = (keep[1] + yr[t][1].astype(F32) + yr[t][2].astype(F32)).reshape(NZ, sub, task_count)
         zt[...] = total
         zs[t][...] = total.astype(Z_TYPES[t])
         z_copies = []
-        for d in range(1, NZ):
+        for d in FAR_FIRST:
             zz = lax.rem(z + d, NZ)
             z_copies.append(send(zs[t].at[zz], zr[t].at[d - 1], {"z": zz}))
         if t == 0:
@@ -227,51 +255,63 @@
         residual = (target_float - fitted).astype(BF16)
         R[t, c, y, z] = residual
         own_rows = R.at[t, c, y, z]
-        r_copies = [send(own_rows, own_rows, {"z": lax.rem(z + d, NZ)}) for d in range(1, NZ)]
+        r_copies = [send(own_rows, own_rows, {"z": lax.rem(z + d, NZ)}) for d in FAR_FIRST]
         resid_float = residual.astype(F32)
         rr.append(jnp.sum(resid_float * resid_float, axis=0, keepdims=True))
         ry.append(jnp.sum(resid_float * target_float, axis=0, keepdims=True))
+        near_first = (0, *reversed(FAR_FIRST))
+        g1, g2 = [], []
+        for d in near_first:
+            if d:
+                r_copies[FAR_FIRST.index(d)].wait_recv()
+            through = R.at[t, c, y, lax.rem(z - d + NZ, NZ)]
+            g1.append(send(through, through, {"y": yf}))
+            g2.append(send(through, through, {"y": yb}))
+
+        def block_to(yy, device):
+            return send(R.at[t, c, yy], R.at[t, c, yy], device)
+
+        R_t = R.at[t]
+        q0 = block_to(y, {"c": oc})
         if t == 0:
             waited(pen_copies)
             pen_src[1] = maximum_of(pen_src[0], pen_z)
             pen_copies = to_all(pen_src.at[1], pen_y, "y", y, NY)
-        waited(r_copies)
-
-        def block_to(yy, device):
-            return send(R.at[t, c, yy], R.at[t, c, yy], device)
-
-        R_t = R.at[t]
-        g1 = block_to(y, {"y": yf})
-        g2 = block_to(y, {"y": yb})
-        q0 = block_to(y, {"c": oc})
+        grad_block(R_t, c, y, True)
+        q0.wait_recv()
+        grad_block(R_t, oc, y, False)
+        g3 = []
+        for d, copy in zip(near_first, g1):
+            copy.wait_recv()
+            through = R.at[t, c, yb, lax.rem(z - d + NZ, NZ)]
+            g3.append(send(through, through, {"y": yf}))
+        q1 = block_to(yb, {"c": oc})
+        waited(g2)
+        q2 = block_to(yf, {"c": oc})
         if t == 0:
             waited(pen_copies)
             pen_src[2] = maximum_of(pen_src[1], pen_y)
             pen_copies = to_all(pen_src.at[2], pen_c, "c", c, 2)
-        grad_block(R_t, c, y, True)
-        q0.wait_recv()
-        grad_block(R_t, oc, y, False)
-        g1.wait_recv()
-        g3 = block_to(yb, {"y": yf})
-        q1 = block_to(yb, {"c": oc})
-        g2.wait_recv()
-        q2 = block_to(yf, {"c": oc})
-        if t == 0:
-            waited(pen_copies)
-            pen_src[3] = maximum_of(pen_src[2], pen_c)
-            pen_copies = to_all(pen_src.at[3], pen_x, "x", x, NX)
         grad_block(R_t, c, yb, False)
         grad_block(R_t, c, yf, False)
         q1.wait_recv()
         grad_block(R_t, oc, yf, False)
-        g3.wait_recv()
-        q3 = block_to(y2, {"c": oc})
+        q3 = []
+        for d, copy in zip(near_first, g3):
+            copy.wait_recv()
+            through = R.at[t, c, y2, lax.rem(z - d + NZ, NZ)]
+            q3.append(send(through, through, {"c": oc}))
         q2.wait_recv()
         grad_block(R_t, oc, yb, False)
         grad_block(R_t, c, y2, False)
-        q3.wait_recv()
+        waited(q3)
         grad_block(R_t, oc, y2, False)
         ga, gb = ring_start(t)
+        if t == 0:
+            waited(pen_copies)
+            pen_src[3] = maximum_of(pen_src[2], pen_c)
+            pen_copies = to_all(pen_src.at[3], pen_x, "x", x, NX)
+        gc = ring_middle(t, ga)
         if t == 0:
             waited(pen_copies)
             pen_max = jnp.max(maximum_of(pen_src[3], pen_x), axis=(0, 1), keepdims=True)
@@ -279,7 +319,6 @@
             waited(square_copies)
             total_squares = (cqs[x] + cqr[0] + cqr[1] + cqr[2])[0:1, :]
             step_sizes = 0.5 / (1.0 + total_squares)
-        gc = ring_middle(t, ga)
         gradient = ring_end(t, gb, gc)
         drain()
         grad_norms = column_norms(gradient)
@@ -296,16 +335,19 @@
             flipped = updated.T
             half[t + 1, x] = flipped.astype(BF16)
             own_half = half.at[t + 1, x]
-            h1 = send(own_half, own_half, {"x": xf})
+            h1 = halved(own_half, own_half, {"x": xf}, quarter)
             h2 = send(own_half, own_half, {"x": xb})
             current[...] = updated
             bn.append(column_norms(updated))
             if t == ITERS - 1:
                 coef_parts[x] = flipped
-            h1.wait_recv()
-            h3 = send(half.at[t + 1, xb], half.at[t + 1, xb], {"x": xf})
+            h3 = []
+            for h in range(2):
+                h1[h].wait_recv()
+                through = half.at[t + 1, xb, pl.ds(h * quarter // 2, quarter // 2)]
+                h3.append(send(through, through, {"x": xf}))
             h2.wait_recv()
-            h3.wait_recv()
+            waited(h3)
             if t == ITERS - 1:
                 own_coef = coef_parts.at[x]
                 coef_copies = [send(own_coef, own_coef, {"x": xq}) for xq in (xf, xb, x2)]
@@ -319,39 +361,51 @@
     norms[x, 3:8, :] = jnp.zeros((5, quarter), F32)
     own_norms = norms.at[x]
     norm_copies = [send(own_norms, own_norms, {"x": xq}) for xq in (xf, xb, x2)]
-    fin_src[0] = stats[...]
-    for k, (arrived, axis, me, n) in enumerate(
-        ((fin_x, "x", x, NX), (fin_c, "c", c, 2), (fin_y, "y", y, NY), (fin_z, "z", z, NZ))
-    ):
-        copies = to_all(fin_src.at[k], arrived, axis, me, n)
-        if k == 1:
+    lane = lax.broadcasted_iota(jnp.int32, (24, 128), 1)
+    row = lax.broadcasted_iota(jnp.int32, (24, 128), 0)
+    sums = jnp.sum(stats[...], axis=1, keepdims=True)
+    tops = jnp.max(stats[...], axis=1, keepdims=True)
+    fin_src[0] = jnp.zeros((8, 128), F32)
+    fin_src[1] = jnp.zeros((8, 128), F32)
+    fin_src[0, 0:1, :] = jnp.sum(jnp.where((lane == row) & (row < 16), sums, 0.0), axis=0, keepdims=True)
+    fin_src[0, 1:2, :] = jnp.sum(jnp.where(lane == row - 16, tops, 0.0), axis=0, keepdims=True)
+    for k, (arrived, group) in enumerate(((fin_plane, plane), (fin_column, column))):
+        copies = [send(fin_src.at[k], arrived.at[i], peer) for i, peer in enumerate(group)]
+        if k == 0:
             waited(coef_copies)
             for q in range(NX):
                 coef[q * quarter : (q + 1) * quarter, :] = coef_parts[q]
         waited(copies)
-        sums, tops = fin_src[k, 0:16, :], fin_src[k, 16:24, :]
-        for d in range(n - 1):
-            sums = sums + arrived[d, 0:16, :]
-            tops = jnp.maximum(tops, arrived[d, 16:24, :])
-        if k < 3:
-            fin_src[k + 1, 0:16, :] = sums
-            fin_src[k + 1, 16:24, :] = tops
-    sums = jnp.sum(sums, axis=1, keepdims=True)
-    tops = jnp.max(tops, axis=1, keepdims=True)
+        sums, tops = fin_src[k, 0:1, :], fin_src[k, 1:2, :]
+        for d in range(len(group)):
+            sums = sums + arrived[d, 0:1, :]
+            tops = jnp.maximum(tops, arrived[d, 1:2, :])
+        if k == 0:
+            fin_src[1, 0:1, :] = sums
+            fin_src[1, 1:2, :] = tops
     waited(norm_copies)
     for t in range(ITERS + 1):
-        scale = jnp.maximum(penalty, tops[t : t + 1, :])
+        scale = jnp.maximum(penalty, tops[:, t : t + 1])
         for q in range(NX):
             corr[t : t + 1, q * quarter : (q + 1) * quarter] = norms[q, t : t + 1, :] / scale
-        rr_sum, ry_sum, bn_sum = sums[t : t + 1], sums[3 + t : 4 + t], sums[6 + t : 7 + t]
+        rr_sum, ry_sum, bn_sum = (sums[:, i : i + 1] for i in (t, 3 + t, 6 + t))
         primal = 0.5 * rr_sum + penalty * bn_sum
         ratio = penalty / scale
         dual = ratio * ry_sum - 0.5 * ratio * ratio * rr_sum
         gaps[t] = jnp.sum((primal - dual) / (primal + 1.0))
     for t in range(ITERS):
-        counts[t] = jnp.sum(sums[9 + t : 10 + t])
+        counts[t] = jnp.sum(sums[:, 9 + t : 10 + t])
     drain()
     assert used[0] == send_sem.shape[0], used[0]
+
+
+def hand_over(coef_in, corr_in, gaps_in, counts_in, coef, corr, gaps, counts):
+    coef[...] = coef_in[...]
+    corr[...] = corr_in[...]
+    for t in range(ITERS + 1):
+        gaps[t] = gaps_in[t]
+    for t in range(ITERS):
+        counts[t] = counts_in[t]
 
 
 def local(design, targets, warm_start, active_mask, penalty_index):
@@ -390,44 +444,35 @@
         vmem((1, 8, 128), F32),
         vmem((NX - 1, 8, 128), F32),
         vmem((NX, 8, quarter), F32),
-        vmem((4, 24, 128), F32),
-        vmem((NX - 1, 24, 128), F32),
-        vmem((1, 24, 128), F32),
-        vmem((NY - 1, 24, 128), F32),
-        vmem((NZ - 1, 24, 128), F32),
+        vmem((2, 8, 128), F32),
+        vmem((NX * NY - 1, 8, 128), F32),
+        vmem((2 * NZ - 1, 8, 128), F32),
         vmem((24, 128), F32),
         pltpu.SemaphoreType.DMA((10,)),
-        pltpu.SemaphoreType.DMA((139,)),
-        pltpu.SemaphoreType.DMA((139,)),
+        pltpu.SemaphoreType.DMA((257,)),
+        pltpu.SemaphoreType.DMA((257,)),
     ]
-    return pl.pallas_call(
+    out_shape = (
+        jax.ShapeDtypeStruct((features, tasks), F32),
+        jax.ShapeDtypeStruct((steps, features), F32),
+        jax.ShapeDtypeStruct((steps,), F32),
+        jax.ShapeDtypeStruct((ITERS,), F32),
+    )
+    results = tuple(pl.BlockSpec(memory_space=m) for m in (vmem, vmem, smem, smem))
+    found = pl.pallas_call(
         kernel,
-        out_shape=(
-            jax.ShapeDtypeStruct((features, tasks), F32),
-            jax.ShapeDtypeStruct((steps, features), F32),
-            jax.ShapeDtypeStruct((steps,), F32),
-            jax.ShapeDtypeStruct((ITERS,), F32),
-        ),
-        in_specs=[
-            pl.BlockSpec(memory_space=hbm),
-            pl.BlockSpec(memory_space=hbm),
-            pl.BlockSpec(memory_space=hbm),
-            pl.BlockSpec(memory_space=vmem),
-            pl.BlockSpec(memory_space=vmem),
-            pl.BlockSpec(memory_space=smem),
-        ],
-        out_specs=(
-            pl.BlockSpec(memory_space=vmem),
-            pl.BlockSpec(memory_space=vmem),
-            pl.BlockSpec(memory_space=smem),
-            pl.BlockSpec(memory_space=smem),
-        ),
+        out_shape=out_shape,
+        in_specs=[pl.BlockSpec(memory_space=m) for m in (hbm, hbm, hbm, vmem, vmem, smem)],
+        out_specs=results,
         scratch_shapes=scratch,
         compiler_params=pltpu.CompilerParams(
-            collective_id=0, has_side_effects=True, vmem_limit_bytes=60 * 1024 * 1024
+            collective_id=0, has_side_effects=True, vmem_limit_bytes=56 * 1024 * 1024
         ),
         name="lasso_steps",
     )(design, targets, target_blocks, warm_start, active_mask, penalty_index)
+    return pl.pallas_call(
+        hand_over, out_shape=out_shape, in_specs=list(results), out_specs=results, name="hand_over"
+    )(*found)
 
 
 def solution(mesh):

time: 174 us -> 154 us (0.89)
  Pallas kernels: 167 us -> 153 us
  local copies, waits for them, and re-layouts: 5.52 us -> 0 us
    pallas_call x1 -> x2, Pallas kernels: 167 us -> 153 us  [the longest x1 151 us: local(): pl.pallas_call(kernel, out_shape=out_shape, in_specs=[pl.BlockSpec(memory...]
    unnamed x4 -> x0, local copies, waits for them, and re-layouts: 5.52 us -> none
where the time goes in v2:
time: 154 us
  Pallas kernels  153 us (99%)
    pallas_call x1, Pallas kernels, local(): pl.pallas_call(kernel, out_shape=out_shape, in_specs=[pl.BlockSpec(memory...  151 us

profile of v2, /device:TPU:1, one launch (start us, length us, event | category | flops | bytes accessed | tf_op | source)
XLA Modules:
  0.0 154.1 jit_solution(4935329169778455156)
XLA Ops:
  1.3 150.8 %lasso_steps.1 = (f32[1024,128]{1,0:T(8,128)}, f32[3,1024]{1,0:T(4,128)}, f32[3]{0:T(128)}, f32[2]{0:T(128)}) custom-call(bf16[3584,1024]{1,0:T(8,128)(2,1)} %design.1, bf16[3584,128]{1,0:T(8,128)(2,1)} %targets.1, bf16[64,56,128]{2,1,0:T(8,128)(2,1)} %bitcast.1, f32[1024,128]{1,0:T(8,128)} %warm.1, s32[2,1024]{1,0:T(2,128)} %mask.1, s32[1]{0:T(128)S(6)} %copy.9.penalty_index), custom_call_target="tpu_custom_call" | custom-call | tf_op jit(solution)/shard_map/lasso_steps/pallas_call | solution.py:462
  152.1 1.9 %hand_over.1 = (f32[1024,128]{1,0:T(8,128)}, f32[3,1024]{1,0:T(4,128)}, f32[3]{0:T(128)}, f32[2]{0:T(128)}) custom-call(f32[1024,128]{1,0:T(8,128)} %get-tuple-element.8.coef_in, f32[3,1024]{1,0:T(4,128)} %get-tuple-element.9.corr_in, f32[3]{0:T(128)} %get-tuple-element.10.gaps_in, f32[2]{0:T(128)} %get-tuple-element.11.counts_in), custom_call_target="tpu_custom_call" | custom-call | tf_op jit(solution)/shard_map/hand_over/pallas_call | solution.py:473

commit v3 on v2

--- a/solution.py
+++ b/solution.py
@@ -9,6 +9,7 @@
 ITERS = 2
 NY, NZ, NX = 4, 8, 4
 MESH = pl.DeviceIdType.MESH
+PIECES = 4
 FAR_FIRST = (4, 3, 5, 2, 6, 1, 7)
 F32 = jnp.float32
 BF16 = jnp.bfloat16
@@ -126,18 +127,18 @@
         else:
             G[...] += product
 
-    task_halves = [pl.ds(h * task_count // 2, task_count // 2) for h in range(2)]
+    task_parts = [pl.ds(h * task_count // PIECES, task_count // PIECES) for h in range(PIECES)]
 
     def ring_start(k):
         gs[k][0] = G[:, cols(x2)].astype(X_TYPES[k])
-        a = [send(gs[k].at[0, p], gr[k].at[0, p], {"x": xf}) for p in task_halves]
+        a = [send(gs[k].at[0, p], gr[k].at[0, p], {"x": xf}) for p in task_parts]
         gs[k][1] = G[:, cols(xb)].astype(X_TYPES[k])
         b = send(gs[k].at[1], gr[k].at[1], {"x": xb})
         return a, b
 
     def ring_middle(k, a):
         last = []
-        for copy, p in zip(a, task_halves):
+        for copy, p in zip(a, task_parts):
             copy.wait_recv()
             gs[k][2, p, :] = (G[p, cols(xf)] + gr[k][0, p, :].astype(F32)).astype(X_TYPES[k])
             last.append(send(gs[k].at[2, p], gr[k].at[2, p], {"x": xf}))
@@ -168,8 +169,8 @@
 
         core_copies = []
 
-        def halved(src, dst, device, length):
-            parts = [pl.ds(h * length // 2, length // 2) for h in range(2)]
+        def in_pieces(src, dst, device, length):
+            parts = [pl.ds(h * length // PIECES, length // PIECES) for h in range(PIECES)]
             return [send(src.at[p], dst.at[p], device) for p in parts]
 
         def other(j):
@@ -190,7 +191,7 @@
         other(0)
         other(1)
         ys[t][0] = summed(0).astype(Y_TYPES[t])
-        ya = halved(ys[t].at[0], yr[t].at[0], {"y": yf}, block)
+        ya = in_pieces(ys[t].at[0], yr[t].at[0], {"y": yf}, block)
         other(2)
         ys[t][1] = summed(1).astype(Y_TYPES[t])
         yb_copy = send(ys[t].at[1], yr[t].at[1], {"y": yb})
@@ -211,9 +212,9 @@
                     G[...] += corr_product
             ca, cb = ring_start(ITERS + 1)
         yc = []
-        for h in range(2):
+        for h in range(PIECES):
             ya[h].wait_recv()
-            p = pl.ds(h * block // 2, block // 2)
+            p = pl.ds(h * block // PIECES, block // PIECES)
             ys[t][2, p, :] = (keep[0, p, :] + yr[t][0, p, :].astype(F32)).astype(Y_TYPES[t])
             yc.append(send(ys[t].at[2, p], yr[t].at[2, p], {"y": yf}))
         if t == 0:
@@ -335,16 +336,16 @@
             flipped = updated.T
             half[t + 1, x] = flipped.astype(BF16)
             own_half = half.at[t + 1, x]
-            h1 = halved(own_half, own_half, {"x": xf}, quarter)
+            h1 = in_pieces(own_half, own_half, {"x": xf}, quarter)
             h2 = send(own_half, own_half, {"x": xb})
             current[...] = updated
             bn.append(column_norms(updated))
             if t == ITERS - 1:
                 coef_parts[x] = flipped
             h3 = []
-            for h in range(2):
+            for h in range(PIECES):
                 h1[h].wait_recv()
-                through = half.at[t + 1, xb, pl.ds(h * quarter // 2, quarter // 2)]
+                through = half.at[t + 1, xb, pl.ds(h * quarter // PIECES, quarter // PIECES)]
                 h3.append(send(through, through, {"x": xf}))
             h2.wait_recv()
             waited(h3)
@@ -449,8 +450,8 @@
         vmem((2 * NZ - 1, 8, 128), F32),
         vmem((24, 128), F32),
         pltpu.SemaphoreType.DMA((10,)),
-        pltpu.SemaphoreType.DMA((257,)),
-        pltpu.SemaphoreType.DMA((257,)),
+        pltpu.SemaphoreType.DMA((293,)),
+        pltpu.SemaphoreType.DMA((293,)),
     ]
     out_shape = (
         jax.ShapeDtypeStruct((features, tasks), F32),

time: 154 us -> 153 us (level)
  Pallas kernels: 153 us -> 151 us
where the time goes in v3:
time: 153 us
  Pallas kernels  151 us (99%)
    pallas_call x1, Pallas kernels, local(): pl.pallas_call(kernel, out_shape=out_shape, in_specs=[pl.BlockSpec(memory...  149 us

profile of v3, /device:TPU:1, one launch (start us, length us, event | category | flops | bytes accessed | tf_op | source)
XLA Modules:
  0.0 152.8 jit_solution(6402839836354314637)
XLA Ops:
  1.3 149.4 %lasso_steps.1 = (f32[1024,128]{1,0:T(8,128)}, f32[3,1024]{1,0:T(4,128)}, f32[3]{0:T(128)}, f32[2]{0:T(128)}) custom-call(bf16[3584,1024]{1,0:T(8,128)(2,1)} %design.1, bf16[3584,128]{1,0:T(8,128)(2,1)} %targets.1, bf16[64,56,128]{2,1,0:T(8,128)(2,1)} %bitcast.1, f32[1024,128]{1,0:T(8,128)} %warm.1, s32[2,1024]{1,0:T(2,128)} %mask.1, s32[1]{0:T(128)S(6)} %copy.9.penalty_index), custom_call_target="tpu_custom_call" | custom-call | tf_op jit(solution)/shard_map/lasso_steps/pallas_call | solution.py:463
  150.7 1.9 %hand_over.1 = (f32[1024,128]{1,0:T(8,128)}, f32[3,1024]{1,0:T(4,128)}, f32[3]{0:T(128)}, f32[2]{0:T(128)}) custom-call(f32[1024,128]{1,0:T(8,128)} %get-tuple-element.8.coef_in, f32[3,1024]{1,0:T(4,128)} %get-tuple-element.9.corr_in, f32[3]{0:T(128)} %get-tuple-element.10.gaps_in, f32[2]{0:T(128)} %get-tuple-element.11.counts_in), custom_call_target="tpu_custom_call" | custom-call | tf_op jit(solution)/shard_map/hand_over/pallas_call | solution.py:474
